TPU v7x, 32 devices: a whole 2x2x4 slice. The times are simulated.
32 devices in a mesh: row: 4 (over y, core), col: 8 (over z, x).
Axes of the slice: x: 2, y: 2, z: 4, core: 2. Of those that a mesh axis runs over, the one named last changes fastest.
Arguments:
- amplitudes: float32 [48, 256, 1024], P('col', None, 'row'), may hold values from -6 to 6
- interaction: float32 [8192, 8192], P('row', 'col'), may hold values from -0.5 to 0.5, as said below
- tile_counts: int32 [8], replicated, may hold values from 2 to 6, as said below
- tile_block: int32 [48], replicated, may hold values from -1 to 31, as said below
- recouple_sign: int32 [48], replicated, may hold values from 0 to 1
- orbit_perm: int32 [48, 256], replicated, may hold values from 0 to 255, each once within a row
- particle_energy: float32 [48, 256], P('col'), may hold values from -2 to 2
Outputs:
- sigma: float32 [48, 256, 1024], P('col', None, 'row')
Inputs may be any that keep to these rules, and one draw needn't show every extreme that they name: Owner c holds its live tiles in its first tile_counts[c] slots; the counts sum to 32, and some owner holds 6. `tile_block`: live slots map one to one onto the 32 cross-channel tiles, and slots that are not live hold -1; two live tiles of one owner never lie in the same aligned group of 4 cross-channel tiles. interaction equals its transpose.
All inputs are finite; a program needn't handle non-finite values.
Results may differ from a plain program's by a relative error of at most 0.000061.
Values sent between devices are 32-bit elements; how exact they have to be, the bound alone decides.
No kernel may reach another device: no remote copies, remote signals or barrier semaphores. Data moves between devices by JAX's collectives and lax.ppermute only.
A program may use at most 128 MiB of HBM per device.

v0:
```python
import jax
import jax.numpy as jnp
from jax import lax
from jax.sharding import PartitionSpec as P


def tile_recouple(tiles, phases, orders):
    moved = jax.vmap(lambda single, ordering: jnp.take(single, ordering, axis=0))(tiles, orders)
    return moved * phases[:, None, None]


def local(
    amplitudes, interaction, tile_counts, tile_block, recouple_sign, orbit_perm, particle_energy
):
    column_index = lax.axis_index("col")
    row_index = lax.axis_index("row")
    column_count = lax.axis_size("col")
    slots, tile_rows, narrow_cols = amplitudes.shape
    row_blocks = interaction.shape[0] // tile_rows
    col_blocks = interaction.shape[1] // tile_rows
    tile_total = tile_block.shape[0]
    slot_ids = jnp.arange(slots, dtype=jnp.int32)
    is_live = slot_ids < jnp.take(tile_counts, column_index)
    live_mask = is_live.astype(jnp.float32)[:, None, None]
    own_block = jnp.where(
        is_live, lax.dynamic_slice_in_dim(tile_block, column_index * slots, slots), -1
    )
    all_phases = (1 - 2 * recouple_sign).astype(jnp.float32)
    own_phases = lax.dynamic_slice_in_dim(all_phases, column_index * slots, slots)
    own_orders = lax.dynamic_slice_in_dim(orbit_perm, column_index * slots, slots, 0)
    diagonal = particle_energy[:, :, None] * amplitudes
    tile_ids = jnp.arange(tile_total, dtype=jnp.int32)
    peer_ids = jnp.arange(column_count, dtype=jnp.int32)

    def tiles_of(blocks):
        matches = tile_block[None, :] == blocks[:, None]
        return jnp.sum(jnp.where(matches, tile_ids[None, :], 0), axis=1)

    target_col = own_block // col_blocks
    my_blocks = column_index * col_blocks + jnp.arange(col_blocks, dtype=jnp.int32)
    block_tiles = tiles_of(my_blocks)
    widened = lax.all_gather(amplitudes, "row", axis=2, tiled=True)
    widened = tile_recouple(widened, own_phases, own_orders)
    group_blocks = row_index * row_blocks + jnp.arange(row_blocks, dtype=jnp.int32)
    group_tiles = tiles_of(group_blocks)
    is_owned = group_tiles // slots == column_index
    placed = (
        jnp.take(widened, group_tiles % slots, axis=0) * is_owned.astype(jnp.float32)[:, None, None]
    )
    crossed = lax.psum(placed.reshape(row_blocks * tile_rows, widened.shape[2]), "col")
    partial_cols = lax.dot_general(
        interaction,
        crossed,
        (((0,), (0,)), ((), ())),
        precision=lax.Precision.HIGHEST,
        preferred_element_type=jnp.float32,
    )
    own_part = lax.psum_scatter(partial_cols, "row", scatter_dimension=1, tiled=True)
    blocks_here = own_part.reshape(col_blocks, tile_rows, narrow_cols)
    block_inverse = jnp.argsort(jnp.take(orbit_perm, block_tiles, axis=0), axis=1)
    blocks_here = tile_recouple(blocks_here, jnp.take(all_phases, block_tiles), block_inverse)
    block_owner = block_tiles // slots
    choose_mask = block_owner[None, :] == peer_ids[:, None]
    choose_block = jnp.sum(
        jnp.where(choose_mask, jnp.arange(col_blocks, dtype=jnp.int32)[None, :], 0), axis=1
    )
    choose_weight = jnp.max(choose_mask.astype(jnp.float32), axis=1)
    outgoing = jnp.take(blocks_here, choose_block, axis=0) * choose_weight[:, None, None]
    arrived = lax.all_to_all(outgoing, "col", split_axis=0, concat_axis=0, tiled=True)
    returned = jnp.take(arrived, jnp.clip(target_col, 0, column_count - 1), axis=0)
    return (returned + diagonal) * live_mask


def solution(mesh):
    placed = (P("col", None, "row"), P("row", "col"), P(), P(), P(), P(), P("col", None))
    return jax.shard_map(
        local, mesh=mesh, in_specs=placed, out_specs=P("col", None, "row"), check_vma=False
    )
```

profile of v0, /device:TPU:0, one launch (start us, length us, event | category | flops | bytes accessed | tf_op | source)
XLA Modules:
  0.0 530.0 jit_solution(5683541795034638029)
XLA Ops:
  7.4 0.7 all-gather.2.cloned.1.call-update
  8.1 0.7 subtract_convert_fusion
  8.9 0.7 bitcast_or_fusion
  9.6 0.8 select_reduce_fusion
  10.7 0.7 compare_and_fusion
  11.4 47.4 %all-gather.2.cloned.1.call-done = f32[6,256,1024]{2,1,0:T(8,128)} async-done(((f32[6,256,256]{2,1,0:T(8,128)}), f32[6,256,1024]{2,1,0:T(8,128)}) %all-gather.2.cloned.1.call-update) | async-done | bytes 6291472 | tf_op jit(solution)/shard_map/all_gather | solution.py:42
  58.8 30.4 %gather_fusion.5 = f32[1536,1024]{1,0:T(8,128)} fusion(f32[6,256,1024]{2,1,0:T(8,128)} %all-gather.2.cloned.1.call-done, s32[1536]{0:T(1024)S(1)} %reshape.217), kind=kCustom, calls=%fused_computation.5 | custom fusion | bytes 12595200 | tf_op jit(solution)/shard_map/vmap(jit(_take))/gather | solution.py:8
  89.3 4.9 select_multiply_fusion
  94.2 7.1 %gather_fusion.1 = f32[8,256,1024]{2,1,0:T(8,128)} fusion(f32[6,256,1024]{2,1,0:T(8,128)} %select_multiply_fusion, s32[1024]{0:T(1024)S(1)} %pad_clamp_fusion.2), kind=kCustom, calls=%fused_computation.1 | custom fusion | bytes 16777248 | tf_op jit(solution)/shard_map/jit(_take)/gather | solution.py:48
  101.2 5.8 %fusion = f32[2048,1024]{1,0:T(8,128)} fusion(f32[8,256,1024]{2,1,0:T(8,128)} %gather_fusion.1, f32[2048]{0:T(1024)S(1)} %bitcast.44, pred[2048]{0:T(1024)(128)(4,1)S(1)} %broadcast_in_dim.145), kind=kLoop, calls=%fused_computation.8 | loop fusion | flops 4194304 | bytes 16787456 | tf_op jit(solution)/shard_map/mul | solution.py:48
  107.2 0.6 copy-done.2
  107.7 0.2 select_reduce_fusion.2
  107.9 0.6 gather_fusion.2
  108.6 0.6 gather_fusion
  109.2 0.7 broadcast_select_fusion
  109.8 0.6 iota.37
  110.4 0.2 reduce-scatter.2.cloned.1.call-start
  110.7 266.6 %all-reduce.2.cloned.1.call-done = f32[2048,1024]{1,0:T(8,128)} async-done(((f32[2048,1024]{1,0:T(8,128)}), f32[2048,1024]{1,0:T(8,128)}) %all-reduce.2.cloned.1.call-update) | async-done | bytes 8388624 | tf_op jit(solution)/shard_map/psum | solution.py:50
  377.3 31.6 %convolution_bitcast_fusion = f32[1024,1024]{0,1:T(8,128)} fusion(f32[2048,1024]{1,0:T(8,128)} %all-reduce.2.cloned.1.call-done, f32[2048,1024]{1,0:T(8,128)} %param.8), kind=kOutput, calls=%fused_computation.10 | convolution fusion | flops 25769803776 | bytes 20971520 | tf_op jit(solution)/shard_map/dot_general | solution.py:51
  409.2 0.7 fusion.1
  409.9 0.7 compare_and_fusion.1
  410.6 42.2 %reduce-scatter.2.cloned.1.call-done = f32[1024,256]{0,1:T(8,128)} async-done(((f32[1024,1024]{0,1:T(8,128)}), f32[1024,256]{0,1:T(8,128)}) %reduce-scatter.2.cloned.1.call-update) | async-done | bytes 1048592 | tf_op jit(solution)/shard_map/reduce_scatter | solution.py:58
  452.8 1.6 copy.11
  454.3 7.3 %gather_fusion.6 = f32[1024,256]{1,0:T(8,128)S(1)} fusion(f32[4,256,256]{2,1,0:T(8,128)S(1)} %bitcast.40, s32[1024]{0:T(1024)S(1)} %bitcast.41), kind=kCustom, calls=%fused_computation.6 | custom fusion | bytes 2105344 | tf_op jit(solution)/shard_map/vmap(jit(_take))/gather | solution.py:8
  461.6 0.2 select_multiply_fusion.2
  461.9 0.7 gather_fusion.3
  462.6 1.6 select_multiply_fusion.1
  464.2 5.5 %all-to-all-start = ((f32[8,256,256]{2,1,0:T(8,128)}), f32[8,256,256]{2,1,0:T(8,128)S(1)}, u32[]{:S(2)}, u32[]{:S(2)}) async-start(f32[8,256,256]{2,1,0:T(8,128)} %select_multiply_fusion.1), calls=%async_computation.1 | async-start | bytes 4194304 | tf_op jit(solution)/shard_map/all_to_all | solution.py:69
  469.7 0.6 dynamic-slice.2
  471.1 46.7 %all-to-all-done = f32[8,256,256]{2,1,0:T(8,128)S(1)} async-done(((f32[8,256,256]{2,1,0:T(8,128)}), f32[8,256,256]{2,1,0:T(8,128)S(1)}, u32[]{:S(2)}, u32[]{:S(2)}) %all-to-all-start) | async-done | bytes 2097184 | tf_op jit(solution)/shard_map/all_to_all | solution.py:69
  517.8 1.8 gather_fusion.4
  519.6 3.3 add_multiply_fusion
  (37 shorter events, 0.8 us)
Async XLA Ops:
  7.4 51.5 %all-gather.2.cloned.1.call-start = ((), (), s32[]{:S(2)}) async-start(), calls=%async_computation.2 | async-start | bytes 7864320 | tf_op jit(solution)/shard_map/all_gather | solution.py:42
  8.1 369.2 %all-reduce.2.cloned.1.call-start = ((), (), s32[]{:S(2)}) async-start(), calls=%async_computation.3 | async-start | bytes 16777216 | tf_op jit(solution)/shard_map/psum | solution.py:50
  107.1 0.7 copy-start.2
  107.1 1.5 copy-start
  107.1 302.1 %sort.19.cloned.1.call-start = ((), (), s32[]{:S(2)}) async-start(), calls=%async_computation.5 | async-start | bytes 24608 | tf_op jit(solution)/shard_map/jit(argsort)/sort | solution.py:60
  110.4 342.3 %reduce-scatter.2.cloned.1.call-start = ((), (), s32[]{:S(2)}) async-start(), calls=%async_computation.4 | async-start | bytes 5242880 | tf_op jit(solution)/shard_map/reduce_scatter | solution.py:58
  461.9 7.9 %copy-start.3 = (s32[8]{0:T(128)S(1)}, s32[8]{0:T(128)}, u32[]{:S(2)}) copy-start(s32[8]{0:T(128)} %param.9) | copy-start | bytes 100
  462.6 57.0 %copy-start.1 = (f32[6,256]{1,0:T(8,128)S(1)}, f32[6,256]{1,0:T(8,128)}, u32[]{:S(2)}) copy-start(f32[6,256]{1,0:T(8,128)} %param.13) | copy-start | bytes 18436
  464.2 53.6 %all-to-all-start = ((f32[8,256,256]{2,1,0:T(8,128)}), f32[8,256,256]{2,1,0:T(8,128)S(1)}, u32[]{:S(2)}, u32[]{:S(2)}) async-start(f32[8,256,256]{2,1,0:T(8,128)} %select_multiply_fusion.1), calls=%async_computation.1 | async-start | bytes 4194304 | tf_op jit(solution)/shard_map/all_to_all | solution.py:69
Sparse Core Ops, SparseCore 0:
  9.7 49.0 all-gather.1
  107.2 270.0 all-reduce.1
  409.1 43.6 reduce-scatter.1
Sparse Core Ops, SparseCore 1:
  110.5 2.5 sort.21.cloned.1.call-done
  (1 shorter events, 0.0 us)
where the time goes:
time: 531 us; the launch traced here: 530 us
  waiting for transfers between devices  404 us (76%)
  local copies, waits for them, and re-layouts  52.1 us (10%)
  matrix products  31.6 us (6%)
  other arithmetic  21.4 us (4%)
  between operations  15.3 us (3%)
  starting transfers between devices  5.77 us (1%)
    psum x1, waiting for transfers between devices, local(): lax.psum(placed.reshape(row_blocks * tile_rows, widened.shape[2]), 'col')  267 us
    all_gather x1, waiting for transfers between devices, local(): widened = lax.all_gather(amplitudes, 'row', axis=2, tiled=True)  47.4 us
    all_to_all x1, waiting for transfers between devices, local(): lax.all_to_all(outgoing, 'col', split_axis=0, concat_axis=0, tiled=True)  46.7 us
    reduce_scatter x1, waiting for transfers between devices, local(): lax.psum_scatter(partial_cols, 'row', scatter_dimension=1, tiled=True)  42.2 us
    gather x3, local copies, waits for them, and re-layouts, tile_recouple(): jnp.take(single, ordering, axis=0)  37.7 us
    dot_general x1, matrix products, local(): lax.dot_general(interaction, crossed, (((0,), (0,)), ((), ())), precision...  31.6 us
  transfers between devices with their start and end apart: 4, of which 4 were waited for; matrix products, arithmetic and copies ran while one was open for 2% of the time, Pallas kernels for 0%

commit v1 on v0

--- a/solution.py
+++ b/solution.py
@@ -47,7 +47,9 @@
     placed = (
         jnp.take(widened, group_tiles % slots, axis=0) * is_owned.astype(jnp.float32)[:, None, None]
     )
-    crossed = lax.psum(placed.reshape(row_blocks * tile_rows, widened.shape[2]), "col")
+    crossed = jnp.sum(
+        lax.all_gather(placed.reshape(row_blocks * tile_rows, widened.shape[2]), "col"), axis=0
+    )
     partial_cols = lax.dot_general(
         interaction,
         crossed,

time: 531 us -> 1550 us (2.92)
  waiting for transfers between devices: 404 us -> 1400 us
  other arithmetic: 21.4 us -> 46 us
    all_gather x0 -> x1, waiting for transfers between devices: none -> 1260 us  [local(): lax.all_gather(placed.reshape(row_blocks * tile_rows, widened.shape[2]),...]
    psum x1 -> x0, waiting for transfers between devices: 267 us -> none  [local(): lax.psum(placed.reshape(row_blocks * tile_rows, widened.shape[2]), 'col')]
    reduce_sum x0 -> x1, other arithmetic: none -> 24.5 us  [local(): jnp.sum(lax.all_gather(placed.reshape(row_blocks * tile_rows, widened.sha...]
  transfers between devices with their start and end apart: 4 -> 4, of which waited for: 4 -> 4; matrix products, arithmetic and copies ran while one was open for 2% -> 1% of each run, Pallas kernels for 0% -> 0%
where the time goes in v1:
time: 1550 us
  waiting for transfers between devices  1400 us (90%)
  local copies, waits for them, and re-layouts  52.1 us (3%)
  other arithmetic  46 us (3%)
  matrix products  31.6 us (2%)
    all_gather x1, waiting for transfers between devices, local(): lax.all_gather(placed.reshape(row_blocks * tile_rows, widened.shape[2]),...  1260 us
    all_gather x1, waiting for transfers between devices, local(): widened = lax.all_gather(amplitudes, 'row', axis=2, tiled=True)  47.4 us
    all_to_all x1, waiting for transfers between devices, local(): lax.all_to_all(outgoing, 'col', split_axis=0, concat_axis=0, tiled=True)  46.7 us
    reduce_scatter x1, waiting for transfers between devices, local(): lax.psum_scatter(partial_cols, 'row', scatter_dimension=1, tiled=True)  43.1 us
    gather x3, local copies, waits for them, and re-layouts, tile_recouple(): jnp.take(single, ordering, axis=0)  37.7 us
    dot_general x1, matrix products, local(): lax.dot_general(interaction, crossed, (((0,), (0,)), ((), ())), precision...  31.6 us
  transfers between devices with their start and end apart: 4, of which 4 were waited for; matrix products, arithmetic and copies ran while one was open for 1% of the time, Pallas kernels for 0%

profile of v1, /device:TPU:0, one launch (start us, length us, event | category | flops | bytes accessed | tf_op | source)
XLA Modules:
  0.0 1552.3 jit_solution(3391319183507431112)
XLA Ops:
  7.4 0.7 all-gather.3.cloned.1.call-update
  8.1 0.7 subtract_convert_fusion
  8.9 0.7 bitcast_or_fusion
  9.6 0.8 select_reduce_fusion
  10.7 0.7 compare_and_fusion
  11.4 47.4 %all-gather.3.cloned.1.call-done = f32[6,256,1024]{2,1,0:T(8,128)} async-done(((f32[6,256,256]{2,1,0:T(8,128)}), f32[6,256,1024]{2,1,0:T(8,128)}) %all-gather.3.cloned.1.call-update) | async-done | bytes 6291472 | tf_op jit(solution)/shard_map/all_gather | solution.py:42
  58.8 30.4 %gather_fusion.5 = f32[1536,1024]{1,0:T(8,128)} fusion(f32[6,256,1024]{2,1,0:T(8,128)} %all-gather.3.cloned.1.call-done, s32[1536]{0:T(1024)S(1)} %reshape.270), kind=kCustom, calls=%fused_computation.5 | custom fusion | bytes 12595200 | tf_op jit(solution)/shard_map/vmap(jit(_take))/gather | solution.py:8
  89.3 4.9 select_multiply_fusion
  94.2 7.1 gather_fusion.1
  101.2 5.8 fusion
  107.1 0.6 copy-done.2
  107.9 0.6 gather_fusion.2
  108.5 0.6 gather_fusion
  109.1 0.7 broadcast_select_fusion
  109.8 0.6 iota.37
  110.4 0.2 reduce-scatter.2.cloned.1.call-start
  110.6 1263.5 %all-gather.5.cloned.1.call-done = f32[8,2048,1024]{2,1,0:T(8,128)} async-done(((f32[1,2048,1024]{2,1,0:T(8,128)}), f32[8,2048,1024]{2,1,0:T(8,128)}) %all-gather.5.cloned.1.call-update) | async-done | bytes 67108880 | tf_op jit(solution)/shard_map/all_gather | solution.py:51
  1374.1 24.5 %reduce_sum.44 = f32[2048,1024]{1,0:T(8,128)} reduce(f32[8,2048,1024]{2,1,0:T(8,128)} %all-gather.5.cloned.1.call-done, f32[]{:T(128)} %constant.163.clone.1), dimensions={0}, to_apply=%region_4.5 | reduce | flops 14680064 | bytes 75497472 | tf_op jit(solution)/shard_map/reduce_sum | solution.py:50
  1398.6 31.6 %convolution_bitcast_fusion = f32[1024,1024]{0,1:T(8,128)} fusion(f32[2048,1024]{1,0:T(8,128)} %reduce_sum.44, f32[2048,1024]{1,0:T(8,128)} %param.8), kind=kOutput, calls=%fused_computation.10 | convolution fusion | flops 25769803776 | bytes 20971520 | tf_op jit(solution)/shard_map/dot_general | solution.py:53
  1430.5 0.7 fusion.1
  1431.2 0.7 compare_and_fusion.1
  1431.9 43.1 %reduce-scatter.2.cloned.1.call-done = f32[1024,256]{0,1:T(8,128)} async-done(((f32[1024,1024]{0,1:T(8,128)}), f32[1024,256]{0,1:T(8,128)}) %reduce-scatter.2.cloned.1.call-update) | async-done | bytes 1048592 | tf_op jit(solution)/shard_map/reduce_scatter | solution.py:60
  1475.0 1.6 copy.12
  1476.6 7.3 gather_fusion.6
  1483.9 0.2 select_multiply_fusion.2
  1484.1 0.7 gather_fusion.3
  1484.8 1.6 select_multiply_fusion.1
  1486.5 5.5 all-to-all-start
  1492.0 0.6 dynamic-slice.2
  1493.3 46.7 %all-to-all-done = f32[8,256,256]{2,1,0:T(8,128)S(1)} async-done(((f32[8,256,256]{2,1,0:T(8,128)}), f32[8,256,256]{2,1,0:T(8,128)S(1)}, u32[]{:S(2)}, u32[]{:S(2)}) %all-to-all-start) | async-done | bytes 2097184 | tf_op jit(solution)/shard_map/all_to_all | solution.py:71
  1540.0 1.8 gather_fusion.4
  1541.8 3.3 add_multiply_fusion
  (38 shorter events, 1.0 us)
Async XLA Ops:
  7.4 51.5 %all-gather.3.cloned.1.call-start = ((), (), s32[]{:S(2)}) async-start(), calls=%async_computation.2 | async-start | bytes 7864320 | tf_op jit(solution)/shard_map/all_gather | solution.py:42
  8.1 1366.0 %all-gather.5.cloned.1.call-start = ((), (), s32[]{:S(2)}) async-start(), calls=%async_computation.3 | async-start | bytes 75497472 | tf_op jit(solution)/shard_map/all_gather | solution.py:51
  107.0 0.7 copy-start.2
  107.0 1.5 copy-start
  107.1 1323.4 %sort.19.cloned.1.call-start = ((), (), s32[]{:S(2)}) async-start(), calls=%async_computation.5 | async-start | bytes 24608 | tf_op jit(solution)/shard_map/jit(argsort)/sort | solution.py:62
  110.4 1364.6 %reduce-scatter.2.cloned.1.call-start = ((), (), s32[]{:S(2)}) async-start(), calls=%async_computation.4 | async-start | bytes 5242880 | tf_op jit(solution)/shard_map/reduce_scatter | solution.py:60
  1484.1 7.9 copy-start.3
  1484.8 57.0 %copy-start.1 = (f32[6,256]{1,0:T(8,128)S(1)}, f32[6,256]{1,0:T(8,128)}, u32[]{:S(2)}) copy-start(f32[6,256]{1,0:T(8,128)} %param.13) | copy-start | bytes 18436
  1486.5 53.6 %all-to-all-start = ((f32[8,256,256]{2,1,0:T(8,128)}), f32[8,256,256]{2,1,0:T(8,128)S(1)}, u32[]{:S(2)}, u32[]{:S(2)}) async-start(f32[8,256,256]{2,1,0:T(8,128)} %select_multiply_fusion.1), calls=%async_computation.1 | async-start | bytes 4194304 | tf_op jit(solution)/shard_map/all_to_all | solution.py:71
Sparse Core Ops, SparseCore 0:
  9.7 49.0 all-gather.2
  107.2 1266.8 all-gather.4
  1430.4 44.5 reduce-scatter.1
Sparse Core Ops, SparseCore 1:
  110.5 2.5 sort.21.cloned.1.call-done
  (1 shorter events, 0.0 us)
